TPU v7x, 32 devices: a whole 2x2x4 slice. The times are simulated.
32 devices in a mesh: dp: 8 (over z, core), tensor: 4 (over y, x).
Axes of the slice: x: 2, y: 2, z: 4, core: 2. Of those that a mesh axis runs over, the one named last changes fastest.
Arguments:
- tokens: bfloat16 [8192, 2048], P('dp'), may hold values from -6 to 6
- lengths: int32 [8], P('dp'), may hold values from 256 to 1024, as said below
- norm1_gain: bfloat16 [2048], replicated, may hold values from 0.5 to 1.5
- norm1_shift: bfloat16 [2048], replicated, may hold values from -4 to 4
- query_weight: bfloat16 [2048, 2048], P(None, 'tensor'), may hold values from -0.1875 to 0.1875
- query_bias: bfloat16 [2048], P('tensor'), may hold values from -6 to 6
- keyval_weight: bfloat16 [2048, 256], replicated, may hold values from -0.1875 to 0.1875
- value_bias: bfloat16 [128], replicated, may hold values from -6 to 6
- proj_weight: bfloat16 [2048, 2048], P('tensor'), may hold values from -0.5 to 0.5
- proj_bias: bfloat16 [2048], replicated, may hold values from -4 to 4
- norm2_gain: bfloat16 [2048], replicated, may hold values from 0.5 to 1.5
- norm2_shift: bfloat16 [2048], replicated, may hold values from -4 to 4
- up_weight: bfloat16 [2048, 8192], P(None, 'tensor'), may hold values from -0.125 to 0.125
- up_bias: bfloat16 [8192], P('tensor'), may hold values from -6 to 6
- down_weight: bfloat16 [8192, 2048], P('tensor'), may hold values from -0.0625 to 0.0625
- down_bias: bfloat16 [2048], replicated, may hold values from -4 to 4
- cotangent: bfloat16 [8192, 2048], P('dp'), may hold values from -6 to 6
Outputs:
- result: bfloat16 [8192, 2048], P('dp')
- grad_tokens: bfloat16 [8192, 2048], P('dp')
- grad_gain1: float32 [2048], replicated
- grad_shift1: float32 [2048], replicated
- grad_query: float32 [2048, 2048], P(None, 'tensor')
- grad_qbias: float32 [2048], P('tensor')
- grad_keyval: float32 [2048, 256], replicated
- grad_vbias: float32 [128], replicated
- grad_proj: float32 [2048, 2048], P('tensor')
- grad_pbias: float32 [2048], replicated
- grad_gain2: float32 [2048], replicated
- grad_shift2: float32 [2048], replicated
- grad_up: float32 [2048, 8192], P(None, 'tensor')
- grad_upbias: float32 [8192], P('tensor')
- grad_down: float32 [8192, 2048], P('tensor')
- grad_dnbias: float32 [2048], replicated
Inputs may be any that keep to these rules, and one draw needn't show every extreme that they name: `lengths`: valid tokens at the start of each slot; some slot is full (1024) and some holds 256.
All inputs are finite; a program needn't handle non-finite values.
Results may differ from a plain program's by a relative error of at most 0.023.
Values may be sent and summed in bfloat16 or wider, within the bound.
A program may use at most 256 MiB of HBM per device.

v0:
```python
import jax
import jax.numpy as jnp
from jax import lax
from jax.sharding import PartitionSpec as P


def layer_norm(values, gain, shift):
    center = values - jnp.mean(values, axis=-1, keepdims=True)
    scaled = center * lax.rsqrt(jnp.mean(center * center, axis=-1, keepdims=True) + 1e-05)
    return scaled * gain + shift


def gelu_tanh(values):
    return (
        0.5
        * values
        * (1.0 + jnp.tanh(0.7978845608028654 * (values + 0.044715 * values * values * values)))
    )


def contract_rows(left, right):
    return lax.dot_general(
        left, right, (((0,), (0,)), ((), ())), preferred_element_type=jnp.float32
    )


def contract_cols(left, right):
    return lax.dot_general(
        left, right, (((1,), (1,)), ((), ())), preferred_element_type=jnp.float32
    )


def block_scores(query_block, key_rows, offset, length):
    scale = query_block.shape[2] ** (-0.5)
    scores = (
        jnp.einsum("qhd,kd->hqk", query_block, key_rows, preferred_element_type=jnp.float32) * scale
    )
    rows_pos = offset + jnp.arange(query_block.shape[0], dtype=jnp.int32)
    keys_pos = jnp.arange(key_rows.shape[0], dtype=jnp.int32)
    allowed = (keys_pos[None, :] <= rows_pos[:, None]) & (keys_pos[None, :] < length)
    return jnp.where(allowed[None], scores, -1e30)


def attend_forward(queries, key_rows, value_rows, length, block_rows):
    pieces = []
    log_totals = []
    for offset in range(0, queries.shape[0], block_rows):
        query_block = queries[offset : offset + block_rows]
        scores = block_scores(query_block, key_rows, offset, length)
        highest = jnp.max(scores, axis=-1, keepdims=True)
        exponent = jnp.exp(scores - highest)
        normaliser = jnp.sum(exponent, axis=-1, keepdims=True)
        probability = (exponent / normaliser).astype(jnp.bfloat16)
        log_totals.append(highest + jnp.log(normaliser))
        pieces.append(
            jnp.einsum("hqk,kd->qhd", probability, value_rows, preferred_element_type=jnp.float32)
        )
    return (jnp.concatenate(pieces, axis=0), log_totals)


def attend_backward(queries, key_rows, value_rows, length, block_rows, log_totals, grad_heads):
    scale = queries.shape[2] ** (-0.5)
    query_grads = []
    key_grads = jnp.zeros(key_rows.shape, jnp.float32)
    value_grads = jnp.zeros(value_rows.shape, jnp.float32)
    for counter, offset in enumerate(range(0, queries.shape[0], block_rows)):
        query_block = queries[offset : offset + block_rows]
        grad_block = grad_heads[offset : offset + block_rows]
        scores = block_scores(query_block, key_rows, offset, length)
        probability = jnp.exp(scores - log_totals[counter])
        grad_probs = jnp.einsum(
            "qhd,kd->hqk", grad_block, value_rows, preferred_element_type=jnp.float32
        )
        inner = jnp.sum(probability * grad_probs, axis=-1, keepdims=True)
        grad_scores = (probability * (grad_probs - inner)).astype(jnp.bfloat16)
        query_grads.append(
            (
                jnp.einsum("hqk,kd->qhd", grad_scores, key_rows, preferred_element_type=jnp.float32)
                * scale
            ).astype(jnp.bfloat16)
        )
        key_grads = (
            key_grads
            + jnp.einsum(
                "hqk,qhd->kd", grad_scores, query_block, preferred_element_type=jnp.float32
            )
            * scale
        )
        value_grads = value_grads + jnp.einsum(
            "hqk,qhd->kd",
            probability.astype(jnp.bfloat16),
            grad_block,
            preferred_element_type=jnp.float32,
        )
    return (jnp.concatenate(query_grads, axis=0), key_grads, value_grads)


def local(
    tokens,
    lengths,
    norm1_gain,
    norm1_shift,
    query_weight,
    query_bias,
    keyval_weight,
    value_bias,
    proj_weight,
    proj_bias,
    norm2_gain,
    norm2_shift,
    up_weight,
    up_bias,
    down_weight,
    down_bias,
    cotangent,
):
    total_rows = tokens.shape[0]
    slot_count = lengths.shape[0]
    slot_len = total_rows // slot_count
    head_dim = keyval_weight.shape[1] // 2
    heads_here = query_weight.shape[1] // head_dim
    block_rows = min(512, slot_len)
    tokens_wide = tokens.astype(jnp.float32)
    gain1 = norm1_gain.astype(jnp.float32)
    shift1 = norm1_shift.astype(jnp.float32)
    gain2 = norm2_gain.astype(jnp.float32)
    shift2 = norm2_shift.astype(jnp.float32)
    normed1, undo_norm1 = jax.vjp(layer_norm, tokens_wide, gain1, shift1)
    hidden1 = normed1.astype(jnp.bfloat16)
    queries = (
        jnp.dot(hidden1, query_weight, preferred_element_type=jnp.float32)
        + query_bias.astype(jnp.float32)
    ).astype(jnp.bfloat16)
    keyval = jnp.dot(hidden1, keyval_weight, preferred_element_type=jnp.float32)
    key_rows = keyval[:, :head_dim].astype(jnp.bfloat16)
    value_rows = (keyval[:, head_dim:] + value_bias.astype(jnp.float32)).astype(jnp.bfloat16)
    number = 0
    slot_queries = queries.reshape(slot_len, heads_here, head_dim)
    attended, log_totals = attend_forward(
        slot_queries, key_rows, value_rows, lengths[number], block_rows
    )
    saved_totals = [log_totals]
    heads_out = attended.reshape(total_rows, heads_here * head_dim).astype(jnp.bfloat16)
    attn_terms = jnp.dot(heads_out, proj_weight, preferred_element_type=jnp.float32)
    middle = (
        tokens_wide
        + lax.psum(attn_terms.astype(jnp.bfloat16), "tensor").astype(jnp.float32)
        + proj_bias.astype(jnp.float32)
    )
    normed2, undo_norm2 = jax.vjp(layer_norm, middle, gain2, shift2)
    hidden2 = normed2.astype(jnp.bfloat16)
    pre_act = jnp.dot(hidden2, up_weight, preferred_element_type=jnp.float32) + up_bias.astype(
        jnp.float32
    )
    activated = gelu_tanh(pre_act).astype(jnp.bfloat16)
    mlp_terms = jnp.dot(activated, down_weight, preferred_element_type=jnp.float32)
    result = (
        middle
        + lax.psum(mlp_terms.astype(jnp.bfloat16), "tensor").astype(jnp.float32)
        + down_bias.astype(jnp.float32)
    ).astype(jnp.bfloat16)
    positions = jnp.arange(slot_len, dtype=jnp.int32)
    valid = (positions[None, :] < lengths[:, None]).astype(jnp.float32).reshape(total_rows, 1)
    grad_result = cotangent.astype(jnp.float32) * valid
    grad_dnbias = jnp.sum(grad_result, axis=0)
    result_low = grad_result.astype(jnp.bfloat16)
    grad_down = contract_rows(activated, result_low)
    grad_act = contract_cols(result_low, down_weight).astype(jnp.bfloat16)
    gelu_pull = jax.vjp(gelu_tanh, pre_act)[1]
    grad_pre = gelu_pull(grad_act.astype(jnp.float32))[0].astype(jnp.bfloat16)
    grad_upbias = jnp.sum(grad_pre.astype(jnp.float32), axis=0)
    grad_up = contract_rows(hidden2, grad_pre)
    back_terms2 = contract_cols(grad_pre, up_weight)
    mid_from_norm, grad_gain2, grad_shift2 = undo_norm2(
        lax.psum(back_terms2.astype(jnp.bfloat16), "tensor").astype(jnp.float32)
    )
    grad_middle = grad_result + mid_from_norm
    middle_low = grad_middle.astype(jnp.bfloat16)
    grad_pbias = jnp.sum(grad_middle, axis=0)
    grad_proj = contract_rows(heads_out, middle_low)
    grad_heads = contract_cols(middle_low, proj_weight).astype(jnp.bfloat16)
    number = 0
    slot_queries = queries.reshape(slot_len, heads_here, head_dim)
    slot_grads = grad_heads.reshape(slot_len, heads_here, head_dim)
    query_part, key_part, value_part = attend_backward(
        slot_queries,
        key_rows,
        value_rows,
        lengths[number],
        block_rows,
        saved_totals[number],
        slot_grads,
    )
    grad_queries = query_part.reshape(total_rows, heads_here * head_dim)
    grad_kv_rows = jnp.concatenate([key_part, value_part], axis=1).astype(jnp.bfloat16)
    grad_qbias = jnp.sum(grad_queries.astype(jnp.float32), axis=0)
    grad_query = contract_rows(hidden1, grad_queries)
    grad_keyval = contract_rows(hidden1, grad_kv_rows)
    grad_vbias = jnp.sum(grad_kv_rows[:, head_dim:].astype(jnp.float32), axis=0)
    back_terms1 = contract_cols(grad_queries, query_weight) + contract_cols(
        grad_kv_rows, keyval_weight
    )
    tokens_from_norm, grad_gain1, grad_shift1 = undo_norm1(
        lax.psum(back_terms1.astype(jnp.bfloat16), "tensor").astype(jnp.float32)
    )
    grad_tokens = (grad_middle + tokens_from_norm).astype(jnp.bfloat16)
    grad_keyval, grad_vbias = lax.psum((grad_keyval, grad_vbias), ("dp", "tensor"))
    (
        grad_query,
        grad_qbias,
        grad_proj,
        grad_pbias,
        grad_gain1,
        grad_shift1,
        grad_gain2,
        grad_shift2,
        grad_up,
        grad_upbias,
        grad_down,
        grad_dnbias,
    ) = (
        lax.psum(grad_query.astype(jnp.bfloat16), "dp").astype(jnp.float32),
        lax.psum(grad_qbias.astype(jnp.bfloat16), "dp").astype(jnp.float32),
        lax.psum(grad_proj.astype(jnp.bfloat16), "dp").astype(jnp.float32),
        lax.psum(grad_pbias.astype(jnp.bfloat16), "dp").astype(jnp.float32),
        lax.psum(grad_gain1.astype(jnp.bfloat16), "dp").astype(jnp.float32),
        lax.psum(grad_shift1.astype(jnp.bfloat16), "dp").astype(jnp.float32),
        lax.psum(grad_gain2.astype(jnp.bfloat16), "dp").astype(jnp.float32),
        lax.psum(grad_shift2.astype(jnp.bfloat16), "dp").astype(jnp.float32),
        lax.psum(grad_up.astype(jnp.bfloat16), "dp").astype(jnp.float32),
        lax.psum(grad_upbias.astype(jnp.bfloat16), "dp").astype(jnp.float32),
        lax.psum(grad_down.astype(jnp.bfloat16), "dp").astype(jnp.float32),
        lax.psum(grad_dnbias.astype(jnp.bfloat16), "dp").astype(jnp.float32),
    )
    return (
        result,
        grad_tokens,
        grad_gain1,
        grad_shift1,
        grad_query,
        grad_qbias,
        grad_keyval,
        grad_vbias,
        grad_proj,
        grad_pbias,
        grad_gain2,
        grad_shift2,
        grad_up,
        grad_upbias,
        grad_down,
        grad_dnbias,
    )


def solution(mesh):
    in_specs = (
        P("dp", None),
        P("dp"),
        P(),
        P(),
        P(None, "tensor"),
        P("tensor"),
        P(),
        P(),
        P("tensor", None),
        P(),
        P(),
        P(),
        P(None, "tensor"),
        P("tensor"),
        P("tensor", None),
        P(),
        P("dp", None),
    )
    out_specs = (
        P("dp", None),
        P("dp", None),
        P(),
        P(),
        P(None, "tensor"),
        P("tensor"),
        P(),
        P(),
        P("tensor", None),
        P(),
        P(),
        P(),
        P(None, "tensor"),
        P("tensor"),
        P("tensor", None),
        P(),
    )
    return jax.shard_map(local, mesh=mesh, in_specs=in_specs, out_specs=out_specs, check_vma=False)
```

profile of v0, /device:TPU:0, one launch (start us, length us, event | category | flops | bytes accessed | tf_op | source)
XLA Modules:
  0.0 1095.1 jit_solution(10420720279538975203)
XLA Ops:
  8.1 1.2 convert_element_type.214
  9.3 0.7 convert_element_type.216
  10.0 3.0 convert_reduce_fusion
  12.9 3.4 fusion.20
  17.6 2.0 fusion.9
  19.6 2.5 add_convert_fusion.4
  22.2 1.3 fusion.106
  24.1 1.6 fusion.97
  25.7 1.2 fusion.34
  26.9 1.7 fusion.71
  29.0 1.6 fusion.98
  30.6 1.2 fusion.33
  31.8 2.1 fusion.70
  34.1 0.9 copy-done.24
  35.0 4.4 convolution_convert_fusion.4
  39.6 106.3 %all-reduce.9.cloned.1.call-done = bf16[1024,2048]{1,0:T(8,128)(2,1)} async-done(((bf16[1024,2048]{1,0:T(8,128)(2,1)}), bf16[1024,2048]{1,0:T(8,128)(2,1)}) %all-reduce.9.cloned.1.call-update) | async-done | bytes 4194320 | tf_op jit(solution)/shard_map/psum | solution.py:147
  146.0 5.0 fusion.38
  151.0 0.9 copy-done.7
  151.9 2.4 multiply_reduce_fusion
  154.3 13.9 %fusion.91 = f32[1024,2048]{1,0:T(8,128)} fusion(bf16[2048,2048]{1,0:T(8,128)(2,1)} %param.29, f32[2048]{0:T(1024)S(1)} %convert_element_type.225, f32[2048]{0:T(1024)S(1)} %convert_element_type.224, f32[1024]{0:T(1024)S(1)} %fusion.86, bf16[1024,2048]{1,0:T(8,128)(2,1)S(1)} %copy-done.7, bf16[1024,2048]{1,0:T(8,128)(2,1)S(1)} %copy-done.3, ...), kind=kOutput, calls=%fused_computation.145 | convolution fusion | flops 8608808960 | bytes 25198592 | tf_op jit(solution)/shard_map/dot_general | solution.py:152
  168.2 19.2 %fusion.101 = (bf16[2048]{0:T(1024)(128)(2,1)}, bf16[1024,2048]{1,0:T(8,128)(2,1)S(1)}) fusion(bf16[2048,2048]{1,0:T(8,128)(2,1)} %param.31, bf16[1024,2048]{1,0:T(8,128)(2,1)S(1)} %copy-done.15, f32[1024]{0:T(1024)S(1)} %fusion.87, f32[1024,2048]{1,0:T(8,128)} %fusion.91, f32[2048]{0:T(1024)S(1)} %convert_element_type.227), kind=kOutput, calls=%fused_computation.153 | convolution fusion | flops 8654944256 | bytes 25182208 | tf_op jit(solution)/shard_map/dot_general | solution.py:28
  187.4 2.0 copy-done.45
  189.4 12.7 %convolution_convert_fusion.2 = bf16[1024,2048]{1,0:T(8,128)(2,1)} fusion(bf16[1024,2048]{1,0:T(8,128)(2,1)S(1)} %get-tuple-element.58, bf16[2048,2048]{1,0:T(8,128)(2,1)} %param.29), kind=kOutput, calls=%fused_computation.83 | convolution fusion | flops 8592031744 | bytes 16777216 | tf_op jit(solution)/shard_map/dot_general | solution.py:28
  202.3 15.9 %convolution_convert_fusion.3 = bf16[1024,2048]{1,0:T(8,128)(2,1)} fusion(bf16[2048,2048]{1,0:T(8,128)(2,1)} %param.31, f32[1024,2048]{1,0:T(8,128)} %fusion.91, f32[2048]{0:T(1024)S(1)} %convert_element_type.227), kind=kOutput, calls=%fused_computation.84 | convolution fusion | flops 8613003264 | bytes 20979712 | tf_op jit(solution)/shard_map/dot_general | solution.py:156
  218.2 87.8 %all-reduce.11.cloned.1.call-done = bf16[1024,2048]{1,0:T(8,128)(2,1)} async-done(((bf16[1024,2048]{1,0:T(8,128)(2,1)}), bf16[1024,2048]{1,0:T(8,128)(2,1)}) %all-reduce.11.cloned.1.call-update) | async-done | bytes 4194320 | tf_op jit(solution)/shard_map/psum | solution.py:175
  306.0 7.0 fusion.10
  313.1 1.2 copy-done.9
  314.3 5.5 fusion.16
  319.8 5.9 fusion.94
  325.8 2.4 fusion.55
  328.2 0.9 copy-done.10
  329.3 2.4 fusion.25
  331.7 2.5 fusion.27
  334.1 3.3 convolution_bitcast_fusion
  337.4 1.5 fusion.100
  339.0 1.5 fusion.64
  340.5 1.9 fusion.28
  342.5 1.6 convert_reduce_fusion.1
  344.1 2.4 fusion.30
  346.6 0.8 fusion.99
  347.4 1.5 fusion.77
  349.1 2.4 fusion.107
  351.5 3.4 add_convert_fusion.1
  355.0 15.7 %convolution_convert_fusion.1 = bf16[2048,2048]{1,0:T(8,128)(2,1)} fusion(bf16[1024,2048]{1,0:T(8,128)(2,1)} %copy-done.45, f32[2048]{0:T(1024)S(1)} %convert_element_type.225, f32[2048]{0:T(1024)S(1)} %convert_element_type.224, f32[1024]{0:T(1024)S(1)} %fusion.86, bf16[1024,2048]{1,0:T(8,128)(2,1)} %all-reduce.9.cloned.1.call-done, ...), kind=kOutput, calls=%fused_computation.69 | convolution fusion | flops 8613003264 | bytes 21004288 | tf_op jit(solution)/shard_map/dot_general | solution.py:22
  370.7 19.9 %convolution_convert_fusion = bf16[2048,2048]{1,0:T(8,128)(2,1)} fusion(bf16[1024,2048]{1,0:T(8,128)(2,1)S(1)} %copy-done.17, f32[1024]{0:T(1024)S(1)} %fusion.87, f32[1024,2048]{1,0:T(8,128)} %fusion.91, f32[2048]{0:T(1024)S(1)} %convert_element_type.227), kind=kOutput, calls=%fused_computation.68 | convolution fusion | flops 8621391872 | bytes 20983808 | tf_op jit(solution)/shard_map/dot_general | solution.py:22
  390.7 3.8 convolution_convert_fusion.6
  394.5 3.7 convolution_convert_fusion.5
  398.9 40.0 %psum.135 = f32[128]{0:T(128)} all-reduce(f32[128]{0:T(128)S(1)} %get-tuple-element.59), channel_id=1, replica_groups=mesh['dp'=8,'tensor'=4] {'dp','tensor'}, use_global_device_ids=true, to_apply=%region_28.29 | all-reduce | flops 128 | bytes 1024 | tf_op jit(solution)/shard_map/psum | solution.py:207
  438.9 4.9 fusion.82
  443.9 2.8 reduce_sum.266
  446.7 81.6 %all-reduce.17.cloned.1.call-done = (bf16[1024,2048]{1,0:T(8,128)(2,1)}, bf16[1024,2048]{1,0:T(8,128)(2,1)}) async-done(((bf16[1024,2048]{1,0:T(8,128)(2,1)}, bf16[1024,2048]{1,0:T(8,128)(2,1)}), (bf16[1024,2048]{1,0:T(8,128)(2,1)}, bf16[1024,2048]{1,0:T(8,128)(2,1)})) %all-reduce.17.cloned.1.call-update) | async-done | bytes 8388624 | tf_op jit(solution)/shard_map/psum | solution.py:159
  528.3 4.5 fusion.21
  532.8 2.8 reduce_sum.258
  535.7 6.3 fusion.17
  542.0 30.6 %all-reduce = (bf16[2048]{0:T(1024)(128)(2,1)S(1)}, bf16[2048]{0:T(1024)(128)(2,1)S(1)}, bf16[512]{0:T(512)(128)(2,1)S(1)}, bf16[2048]{0:T(1024)(128)(2,1)S(1)},...) all-reduce(bf16[2048]{0:T(1024)(128)(2,1)S(1)} %get-tuple-element.1, ...), channel_id=1, replica_groups=mesh['dp'=8,'tensor'=4] {'dp'}, use_global_device_ids=true, to_apply=%region_19.20 | all-reduce | flops 14848 | bytes 59392 | tf_op jit(solution)/shard_map/psum | solution.py:226
  573.1 0.6 convert_element_type.255
  577.3 13.3 %add_convert_fusion = (bf16[1024,2048]{1,0:T(8,128)(2,1)}, bf16[1024,2048]{1,0:T(8,128)(2,1)}) fusion(f32[1024,2048]{1,0:T(8,128)} %copy-done.10, bf16[1024,2048]{1,0:T(8,128)(2,1)} %param.17, bf16[1024,2048]{1,0:T(8,128)(2,1)} %get-tuple-element.33, f32[1024]{0:T(1024)S(1)} %negate_multiply_fusion, f32[1024]{0:T(1024)S(1)} %multiply_multiply_fusion.2, ...), kind=kLoop, calls=%fused_computation.52 | loop fusion | flops 37748736 | bytes 33595392 | tf_op jit(solution)/shard_map/convert_element_type | solution.py:206
  590.7 354.6 %all-reduce.15.cloned.1.call-done = (bf16[2048,512]{1,0:T(8,128)(2,1)}, bf16[512,2048]{1,0:T(8,128)(2,1)}, bf16[2048,2048]{1,0:T(8,128)(2,1)}, bf16[2048,2048]{1,0:T(8,128)(2,1)}) async-done(((bf16[2048,512]{1,0:T(8,128)(2,1)}, bf16[512,2048]{1,0:T(8,128)(2,1)}, bf16[2048,2048]{1,0:T(8,128)(2,1)}, bf16[2048,2048]{1,0:T(8,128)(2,1)}), (bf16[2048,512]{1,0:T(8,128)(2,1)}, bf16[512,2048]{1,0:T(8,128)(2,1)}, ...) | async-done | bytes 20971536 | tf_op jit(solution)/shard_map/psum | solution.py:222
  945.3 4.2 convert_element_type.258
  949.5 4.1 convert_element_type.262
  953.6 11.9 %convert_element_type.269 = f32[2048,2048]{1,0:T(8,128)} convert(bf16[2048,2048]{1,0:T(8,128)(2,1)} %get-tuple-element.30) | non-fusion elementwise | flops 4194304 | bytes 25165824 | tf_op jit(solution)/shard_map/convert_element_type | solution.py:230
  965.6 11.9 %convert_element_type.272 = f32[2048,2048]{1,0:T(8,128)} convert(bf16[2048,2048]{1,0:T(8,128)(2,1)} %get-tuple-element.31) | non-fusion elementwise | flops 4194304 | bytes 25165824 | tf_op jit(solution)/shard_map/convert_element_type | solution.py:232
  977.5 107.8 %all-reduce.13.cloned.1.call-done = f32[2048,256]{1,0:T(8,128)} async-done(((f32[2048,256]{1,0:T(8,128)}), f32[2048,256]{1,0:T(8,128)}) %all-reduce.13.cloned.1.call-update) | async-done | bytes 2097168 | tf_op jit(solution)/shard_map/psum | solution.py:207
  1085.3 3.0 copy.85
  (146 shorter events, 8.0 us)
Async XLA Ops:
  7.2 27.9 %copy-start = (bf16[512,2048]{1,0:T(8,128)(2,1)S(1)}, bf16[512,2048]{1,0:T(8,128)(2,1)}, u32[]{:S(2)}) copy-start(bf16[512,2048]{1,0:T(8,128)(2,1)} %param.25) | copy-start | bytes 6291460
  7.2 9.8 copy-start.35
  7.2 9.8 copy-start.36
  7.2 138.7 %all-reduce.9.cloned.1.call-start = ((), (), s32[]{:S(2)}) async-start(), calls=%async_computation | async-start | bytes 8388608 | tf_op jit(solution)/shard_map/psum | solution.py:147
  7.3 10.3 copy-start.2
  10.0 9.6 copy-start.43
  12.9 4.1 copy-start.29
  16.4 0.6 copy-start.33
  17.0 0.6 copy-start.31
  17.0 0.6 copy-start.27
  19.6 2.6 copy-start.18
  19.6 2.6 copy-start.22
  22.2 3.5 copy-start.20
  22.2 6.8 copy-start.13
  23.5 5.5 copy-start.11
  25.7 3.3 copy-start.5
  30.6 3.3 copy-start.6
  34.0 1.0 copy-start.24
  34.0 5.5 copy-start.37
  34.1 5.5 copy-start.38
  34.1 5.5 copy-start.39
  34.1 5.5 copy-start.40
  39.5 266.5 %all-reduce.11.cloned.1.call-start = ((), (), s32[]{:S(2)}) async-start(), calls=%async_computation.1 | async-start | bytes 8388608 | tf_op jit(solution)/shard_map/psum | solution.py:175
  146.0 5.0 copy-start.3
  146.0 5.9 copy-start.7
  154.3 13.9 %copy-start.15 = (bf16[1024,2048]{1,0:T(8,128)(2,1)S(1)}, bf16[1024,2048]{1,0:T(8,128)(2,1)}, u32[]{:S(2)}) copy-start(bf16[1024,2048]{1,0:T(8,128)(2,1)} %param.33) | copy-start | bytes 12582916
  187.4 2.0 copy-start.45
  202.2 326.1 %all-reduce.17.cloned.1.call-start = ((), (), s32[]{:S(2)}) async-start(), calls=%async_computation.4 | async-start | bytes 16777216 | tf_op jit(solution)/shard_map/psum | solution.py:159
  306.0 7.1 copy-start.4
  306.0 7.1 copy-start.8
  306.0 8.3 copy-start.9
  313.0 6.8 copy-start.16
  314.3 14.9 %slice-start = ((s8[8388608]{0:T(1024)(128)(4,1)}), s8[4194304]{0:T(1024)(128)(4,1)S(1)}, s32[]{:S(2)}) async-start(s8[8388608]{0:T(1024)(128)(4,1)} %bitcast.107), calls=%async_computation.5 | async-start | bytes 8388608
  319.8 9.4 slice-start.1
  325.7 3.4 copy-start.10
  329.3 9.7 slice-start.2
  331.6 5.8 copy-start.12
  331.6 7.3 slice-start.3
  344.1 3.3 copy-start.14
  344.1 3.3 copy-start.26
  346.6 2.4 copy-start.21
  346.6 2.5 copy-start.44
  348.9 2.6 copy-start.23
  354.9 590.4 %all-reduce.15.cloned.1.call-start = ((), (), s32[]{:S(2)}) async-start(), calls=%async_computation.3 | async-start | bytes 41943040 | tf_op jit(solution)/shard_map/psum | solution.py:222
  354.9 15.8 %copy-start.17 = (bf16[1024,2048]{1,0:T(8,128)(2,1)S(1)}, bf16[1024,2048]{1,0:T(8,128)(2,1)}, u32[]{:S(2)}) copy-start(bf16[1024,2048]{1,0:T(8,128)(2,1)} %param.33) | copy-start | bytes 12582916
  355.0 39.5 %slice-start.4 = ((s8[8388608]{0:T(1024)(128)(4,1)}), s8[4194304]{0:T(1024)(128)(4,1)S(1)}, s32[]{:S(2)}) async-start(s8[8388608]{0:T(1024)(128)(4,1)} %bitcast.111), calls=%async_computation.9 | async-start | bytes 8388608
  370.7 19.9 %copy-start.19 = (bf16[1024,2048]{1,0:T(8,128)(2,1)S(1)}, bf16[1024,2048]{1,0:T(8,128)(2,1)}, u32[]{:S(2)}) copy-start(bf16[1024,2048]{1,0:T(8,128)(2,1)} %copy-done.18) | copy-start | bytes 12582916
  370.7 23.8 %slice-start.5 = ((s8[8388608]{0:T(1024)(128)(4,1)}), s8[4194304]{0:T(1024)(128)(4,1)S(1)}, s32[]{:S(2)}) async-start(s8[8388608]{0:T(1024)(128)(4,1)} %bitcast.111), calls=%async_computation.10 | async-start | bytes 8388608
  390.7 3.8 copy-start.25
  398.2 0.7 copy-start.41
  398.2 130.1 %copy-start.28 = (f32[2048]{0:T(1024)S(1)}, f32[2048]{0:T(1024)}, u32[]{:S(2)}) copy-start(f32[2048]{0:T(1024)} %copy-done.27) | copy-start | bytes 24580
  398.2 130.1 %copy-start.30 = (f32[1024]{0:T(1024)S(1)}, f32[1024]{0:T(1024)}, u32[]{:S(2)}) copy-start(f32[1024]{0:T(1024)} %copy-done.29) | copy-start | bytes 12292
  398.2 687.0 %all-reduce.13.cloned.1.call-start = ((), (), s32[]{:S(2)}) async-start(), calls=%async_computation.2 | async-start | bytes 4194304 | tf_op jit(solution)/shard_map/psum | solution.py:207
  443.8 91.8 %copy-start.34 = (f32[1024]{0:T(1024)S(1)}, f32[1024]{0:T(1024)}, u32[]{:S(2)}) copy-start(f32[1024]{0:T(1024)} %copy-done.33) | copy-start | bytes 12292
  443.9 91.8 %copy-start.32 = (f32[1024]{0:T(1024)S(1)}, f32[1024]{0:T(1024)}, u32[]{:S(2)}) copy-start(f32[1024]{0:T(1024)} %copy-done.31) | copy-start | bytes 12292
  532.8 9.2 copy-start.42
  965.6 122.8 %copy-start.1 = (bf16[512,2048]{1,0:T(8,128)(2,1)S(1)}, bf16[512,2048]{1,0:T(8,128)(2,1)}, u32[]{:S(2)}) copy-start(bf16[512,2048]{1,0:T(8,128)(2,1)} %param.25) | copy-start | bytes 6291460
Sparse Core Ops, SparseCore 0:
  39.6 106.3 all-reduce.8
  202.3 103.6 all-reduce.10
  355.0 173.2 all-reduce.16
  532.3 413.0 all-reduce.14
  950.5 134.7 all-reduce.12
where the time goes:
time: 1100 us
  waiting for transfers between devices  738 us (67%)
  matrix products  148 us (13%)
  other arithmetic  111 us (10%)
  blocking collectives  70.6 us (6%)
  between operations  15.7 us (1%)
  local copies, waits for them, and re-layouts  11.6 us (1%)
    psum x1, waiting for transfers between devices, local(): lax.psum(grad_query.astype(jnp.bfloat16), 'dp').astype(jnp.float32)  355 us
    psum x1, waiting for transfers between devices, local(): lax.psum((grad_keyval, grad_vbias), ('dp', 'tensor'))  108 us
    psum x1, waiting for transfers between devices, local(): lax.psum(attn_terms.astype(jnp.bfloat16), 'tensor').astype(jnp.float32)  106 us
    psum x1, waiting for transfers between devices, local(): lax.psum(back_terms2.astype(jnp.bfloat16), 'tensor').astype(jnp.float32)  87.8 us
    psum x1, waiting for transfers between devices, local(): lax.psum(mlp_terms.astype(jnp.bfloat16), 'tensor').astype(jnp.float32)  81.6 us
    dot_general x5, matrix products, contract_rows(): lax.dot_general(left, right, (((0,), (0,)), ((), ())), preferred_element_...  48 us
    dot_general x5, matrix products, contract_cols(): lax.dot_general(left, right, (((1,), (1,)), ((), ())), preferred_element_...  40.2 us
    psum x1, blocking collectives, local(): lax.psum((grad_keyval, grad_vbias), ('dp', 'tensor'))  40 us
  transfers between devices with their start and end apart: 5, of which 5 were waited for; matrix products, arithmetic and copies ran while one was open for 12% of the time, Pallas kernels for 0%

commit v1 on v0

--- a/solution.py
+++ b/solution.py
@@ -172,7 +172,9 @@
     grad_up = contract_rows(hidden2, grad_pre)
     back_terms2 = contract_cols(grad_pre, up_weight)
     mid_from_norm, grad_gain2, grad_shift2 = undo_norm2(
-        lax.psum(back_terms2.astype(jnp.bfloat16), "tensor").astype(jnp.float32)
+        jnp.sum(lax.all_gather(back_terms2.astype(jnp.bfloat16), "tensor"), axis=0).astype(
+            jnp.float32
+        )
     )
     grad_middle = grad_result + mid_from_norm
     middle_low = grad_middle.astype(jnp.bfloat16)

time: 1100 us -> 1160 us (1.055)
  waiting for transfers between devices: 738 us -> 785 us
  other arithmetic: 111 us -> 131 us
    all_gather x0 -> x1, waiting for transfers between devices: none -> 141 us  [local(): lax.all_gather(back_terms2.astype(jnp.bfloat16), 'tensor')]
    psum x1 -> x0, waiting for transfers between devices: 87.8 us -> none  [local(): lax.psum(back_terms2.astype(jnp.bfloat16), 'tensor').astype(jnp.float32)]
    reduce_sum x0 -> x1, other arithmetic: none -> 12.1 us  [local(): jnp.sum(lax.all_gather(back_terms2.astype(jnp.bfloat16), 'tensor'), axis=0)]
where the time goes in v1:
time: 1160 us
  waiting for transfers between devices  785 us (68%)
  matrix products  147 us (13%)
  other arithmetic  131 us (11%)
  blocking collectives  70.6 us (6%)
  between operations  15.7 us (1%)
    psum x1, waiting for transfers between devices, local(): lax.psum(grad_query.astype(jnp.bfloat16), 'dp').astype(jnp.float32)  355 us
    all_gather x1, waiting for transfers between devices, local(): lax.all_gather(back_terms2.astype(jnp.bfloat16), 'tensor')  141 us
    psum x1, waiting for transfers between devices, local(): lax.psum((grad_keyval, grad_vbias), ('dp', 'tensor'))  108 us
    psum x1, waiting for transfers between devices, local(): lax.psum(attn_terms.astype(jnp.bfloat16), 'tensor').astype(jnp.float32)  106 us
    psum x1, waiting for transfers between devices, local(): lax.psum(mlp_terms.astype(jnp.bfloat16), 'tensor').astype(jnp.float32)  74.3 us
    dot_general x5, matrix products, contract_rows(): lax.dot_general(left, right, (((0,), (0,)), ((), ())), preferred_element_...  48.1 us
    dot_general x5, matrix products, contract_cols(): lax.dot_general(left, right, (((1,), (1,)), ((), ())), preferred_element_...  40.2 us
    psum x1, blocking collectives, local(): lax.psum((grad_keyval, grad_vbias), ('dp', 'tensor'))  40 us
  transfers between devices with their start and end apart: 5, of which 5 were waited for; matrix products, arithmetic and copies ran while one was open for 12% of the time, Pallas kernels for 0%

profile of v1, /device:TPU:0, one launch (start us, length us, event | category | flops | bytes accessed | tf_op | source)
XLA Modules:
  0.0 1160.9 jit_solution(1655271433448474885)
XLA Ops:
  8.1 1.2 convert_element_type.216
  9.3 0.7 convert_element_type.218
  10.0 3.0 convert_reduce_fusion
  12.9 3.4 fusion.20
  17.6 2.0 fusion.9
  19.6 2.5 add_convert_fusion.4
  22.2 1.3 fusion.106
  24.1 1.6 fusion.97
  25.7 1.2 fusion.34
  26.9 1.7 fusion.71
  29.0 1.6 fusion.98
  30.6 1.2 fusion.33
  31.8 2.1 fusion.70
  34.1 0.9 copy-done.24
  35.0 4.4 convolution_convert_fusion.4
  39.6 106.3 %all-reduce.8.cloned.1.call-done = bf16[1024,2048]{1,0:T(8,128)(2,1)} async-done(((bf16[1024,2048]{1,0:T(8,128)(2,1)}), bf16[1024,2048]{1,0:T(8,128)(2,1)}) %all-reduce.8.cloned.1.call-update) | async-done | bytes 4194320 | tf_op jit(solution)/shard_map/psum | solution.py:147
  145.9 5.0 fusion.38
  151.0 0.9 copy-done.7
  151.9 2.4 multiply_reduce_fusion
  154.3 13.9 %fusion.91 = f32[1024,2048]{1,0:T(8,128)} fusion(bf16[2048,2048]{1,0:T(8,128)(2,1)} %param.29, f32[2048]{0:T(1024)S(1)} %convert_element_type.227, f32[2048]{0:T(1024)S(1)} %convert_element_type.226, f32[1024]{0:T(1024)S(1)} %fusion.86, bf16[1024,2048]{1,0:T(8,128)(2,1)S(1)} %copy-done.7, bf16[1024,2048]{1,0:T(8,128)(2,1)S(1)} %copy-done.3, ...), kind=kOutput, calls=%fused_computation.145 | convolution fusion | flops 8608808960 | bytes 25198592 | tf_op jit(solution)/shard_map/dot_general | solution.py:152
  168.2 19.2 %fusion.101 = (bf16[2048]{0:T(1024)(128)(2,1)}, bf16[1024,2048]{1,0:T(8,128)(2,1)S(1)}) fusion(bf16[2048,2048]{1,0:T(8,128)(2,1)} %param.31, bf16[1024,2048]{1,0:T(8,128)(2,1)S(1)} %copy-done.15, f32[1024]{0:T(1024)S(1)} %fusion.87, f32[1024,2048]{1,0:T(8,128)} %fusion.91, f32[2048]{0:T(1024)S(1)} %convert_element_type.229), kind=kOutput, calls=%fused_computation.153 | convolution fusion | flops 8654944256 | bytes 25182208 | tf_op jit(solution)/shard_map/dot_general | solution.py:28
  187.4 2.0 copy-done.45
  189.4 12.7 %convolution_convert_fusion.2 = bf16[1024,2048]{1,0:T(8,128)(2,1)} fusion(bf16[1024,2048]{1,0:T(8,128)(2,1)S(1)} %get-tuple-element.58, bf16[2048,2048]{1,0:T(8,128)(2,1)} %param.29), kind=kOutput, calls=%fused_computation.83 | convolution fusion | flops 8592031744 | bytes 16777216 | tf_op jit(solution)/shard_map/dot_general | solution.py:28
  202.3 15.9 %convolution_convert_fusion.3 = bf16[1024,2048]{1,0:T(8,128)(2,1)} fusion(bf16[2048,2048]{1,0:T(8,128)(2,1)} %param.31, f32[1024,2048]{1,0:T(8,128)} %fusion.91, f32[2048]{0:T(1024)S(1)} %convert_element_type.229), kind=kOutput, calls=%fused_computation.84 | convolution fusion | flops 8613003264 | bytes 20979712 | tf_op jit(solution)/shard_map/dot_general | solution.py:156
  218.2 141.4 %all-gather.3.cloned.1.call-done = bf16[4096,2048]{1,0:T(8,128)(2,1)} async-done(((bf16[1024,2048]{1,0:T(8,128)(2,1)}), bf16[4096,2048]{1,0:T(8,128)(2,1)}) %all-gather.3.cloned.1.call-update) | async-done | bytes 16777232 | tf_op jit(solution)/shard_map/all_gather | solution.py:175
  359.6 12.1 %reduce_sum.263 = bf16[1024,2048]{1,0:T(8,128)(2,1)} reduce(bf16[4,1024,2048]{2,1,0:T(8,128)(2,1)} %bitcast.112, bf16[]{:T(256)} %constant.38.clone.1), dimensions={0}, to_apply=%region_10.11 | reduce | flops 6291456 | bytes 20971522 | tf_op jit(solution)/shard_map/reduce_sum | solution.py:175
  371.7 7.2 fusion.10
  379.0 1.0 copy-done.9
  380.1 5.5 fusion.16
  385.6 6.3 fusion.94
  391.9 2.4 fusion.55
  394.4 0.9 copy-done.10
  395.4 2.0 fusion.25
  397.4 2.5 fusion.27
  399.9 3.3 convolution_bitcast_fusion
  403.2 1.5 fusion.100
  404.7 1.5 fusion.64
  406.3 1.9 fusion.28
  408.2 1.6 convert_reduce_fusion.1
  409.9 2.4 fusion.30
  412.4 0.8 fusion.99
  413.2 1.5 fusion.77
  414.8 2.4 fusion.107
  417.3 3.4 add_convert_fusion.1
  420.8 15.7 %convolution_convert_fusion.1 = bf16[2048,2048]{1,0:T(8,128)(2,1)} fusion(bf16[1024,2048]{1,0:T(8,128)(2,1)} %copy-done.45, f32[2048]{0:T(1024)S(1)} %convert_element_type.227, f32[2048]{0:T(1024)S(1)} %convert_element_type.226, f32[1024]{0:T(1024)S(1)} %fusion.86, bf16[1024,2048]{1,0:T(8,128)(2,1)} %all-reduce.8.cloned.1.call-done, ...), kind=kOutput, calls=%fused_computation.69 | convolution fusion | flops 8613003264 | bytes 21004288 | tf_op jit(solution)/shard_map/dot_general | solution.py:22
  436.5 19.9 %convolution_convert_fusion = bf16[2048,2048]{1,0:T(8,128)(2,1)} fusion(bf16[1024,2048]{1,0:T(8,128)(2,1)S(1)} %copy-done.17, f32[1024]{0:T(1024)S(1)} %fusion.87, f32[1024,2048]{1,0:T(8,128)} %fusion.91, f32[2048]{0:T(1024)S(1)} %convert_element_type.229), kind=kOutput, calls=%fused_computation.68 | convolution fusion | flops 8621391872 | bytes 20983808 | tf_op jit(solution)/shard_map/dot_general | solution.py:22
  456.5 3.8 convolution_convert_fusion.6
  460.3 3.7 convolution_convert_fusion.5
  464.7 40.0 %psum.127 = f32[128]{0:T(128)} all-reduce(f32[128]{0:T(128)S(1)} %get-tuple-element.59), channel_id=1, replica_groups=mesh['dp'=8,'tensor'=4] {'dp','tensor'}, use_global_device_ids=true, to_apply=%region_28.29 | all-reduce | flops 128 | bytes 1024 | tf_op jit(solution)/shard_map/psum | solution.py:209
  504.7 4.9 fusion.82
  509.6 10.1 reduce_sum.279
  519.8 74.3 %all-reduce.14.cloned.1.call-done = (bf16[1024,2048]{1,0:T(8,128)(2,1)}, bf16[1024,2048]{1,0:T(8,128)(2,1)}) async-done(((bf16[1024,2048]{1,0:T(8,128)(2,1)}, bf16[1024,2048]{1,0:T(8,128)(2,1)}), (bf16[1024,2048]{1,0:T(8,128)(2,1)}, bf16[1024,2048]{1,0:T(8,128)(2,1)})) %all-reduce.14.cloned.1.call-update) | async-done | bytes 8388624 | tf_op jit(solution)/shard_map/psum | solution.py:159
  594.1 4.5 fusion.21
  598.6 2.8 reduce_sum.271
  601.5 6.3 fusion.17
  607.8 30.6 %all-reduce = (bf16[2048]{0:T(1024)(128)(2,1)S(1)}, bf16[2048]{0:T(1024)(128)(2,1)S(1)}, bf16[512]{0:T(512)(128)(2,1)S(1)}, bf16[2048]{0:T(1024)(128)(2,1)S(1)},...) all-reduce(bf16[2048]{0:T(1024)(128)(2,1)S(1)} %get-tuple-element.1, ...), channel_id=1, replica_groups=mesh['dp'=8,'tensor'=4] {'dp'}, use_global_device_ids=true, to_apply=%region_19.20 | all-reduce | flops 14848 | bytes 59392 | tf_op jit(solution)/shard_map/psum | solution.py:228
  643.1 13.3 %add_convert_fusion = (bf16[1024,2048]{1,0:T(8,128)(2,1)}, bf16[1024,2048]{1,0:T(8,128)(2,1)}) fusion(f32[1024,2048]{1,0:T(8,128)} %copy-done.10, bf16[1024,2048]{1,0:T(8,128)(2,1)} %param.17, bf16[1024,2048]{1,0:T(8,128)(2,1)} %get-tuple-element.33, f32[1024]{0:T(1024)S(1)} %negate_multiply_fusion, f32[1024]{0:T(1024)S(1)} %multiply_multiply_fusion.2, ...), kind=kLoop, calls=%fused_computation.52 | loop fusion | flops 37748736 | bytes 33595392 | tf_op jit(solution)/shard_map/convert_element_type | solution.py:208
  656.5 354.6 %all-reduce.12.cloned.1.call-done = (bf16[2048,512]{1,0:T(8,128)(2,1)}, bf16[512,2048]{1,0:T(8,128)(2,1)}, bf16[2048,2048]{1,0:T(8,128)(2,1)}, bf16[2048,2048]{1,0:T(8,128)(2,1)}) async-done(((bf16[2048,512]{1,0:T(8,128)(2,1)}, bf16[512,2048]{1,0:T(8,128)(2,1)}, bf16[2048,2048]{1,0:T(8,128)(2,1)}, bf16[2048,2048]{1,0:T(8,128)(2,1)}), (bf16[2048,512]{1,0:T(8,128)(2,1)}, bf16[512,2048]{1,0:T(8,128)(2,1)}, ...) | async-done | bytes 20971536 | tf_op jit(solution)/shard_map/psum | solution.py:224
  1011.1 4.2 convert_element_type.260
  1015.3 4.1 convert_element_type.264
  1019.4 11.9 %convert_element_type.271 = f32[2048,2048]{1,0:T(8,128)} convert(bf16[2048,2048]{1,0:T(8,128)(2,1)} %get-tuple-element.30) | non-fusion elementwise | flops 4194304 | bytes 25165824 | tf_op jit(solution)/shard_map/convert_element_type | solution.py:232
  1031.3 11.9 %convert_element_type.274 = f32[2048,2048]{1,0:T(8,128)} convert(bf16[2048,2048]{1,0:T(8,128)(2,1)} %get-tuple-element.31) | non-fusion elementwise | flops 4194304 | bytes 25165824 | tf_op jit(solution)/shard_map/convert_element_type | solution.py:234
  1043.2 107.8 %all-reduce.10.cloned.1.call-done = f32[2048,256]{1,0:T(8,128)} async-done(((f32[2048,256]{1,0:T(8,128)}), f32[2048,256]{1,0:T(8,128)}) %all-reduce.10.cloned.1.call-update) | async-done | bytes 2097168 | tf_op jit(solution)/shard_map/psum | solution.py:209
  1151.1 3.0 copy.84
  (147 shorter events, 8.6 us)
Async XLA Ops:
  7.2 27.9 %copy-start = (bf16[512,2048]{1,0:T(8,128)(2,1)S(1)}, bf16[512,2048]{1,0:T(8,128)(2,1)}, u32[]{:S(2)}) copy-start(bf16[512,2048]{1,0:T(8,128)(2,1)} %param.25) | copy-start | bytes 6291460
  7.2 9.8 copy-start.35
  7.2 9.8 copy-start.36
  7.2 138.7 %all-reduce.8.cloned.1.call-start = ((), (), s32[]{:S(2)}) async-start(), calls=%async_computation | async-start | bytes 8388608 | tf_op jit(solution)/shard_map/psum | solution.py:147
  7.3 10.3 copy-start.2
  10.0 9.6 copy-start.43
  12.9 4.1 copy-start.29
  16.4 0.6 copy-start.33
  17.0 0.6 copy-start.31
  17.0 0.6 copy-start.27
  19.6 2.6 copy-start.18
  19.6 2.6 copy-start.22
  22.2 3.5 copy-start.20
  22.2 6.8 copy-start.13
  23.5 5.5 copy-start.11
  25.7 3.3 copy-start.5
  30.6 3.3 copy-start.6
  34.0 1.0 copy-start.24
  34.0 5.5 copy-start.37
  34.1 5.5 copy-start.38
  34.1 5.5 copy-start.39
  34.1 5.5 copy-start.40
  39.5 320.2 %all-gather.3.cloned.1.call-start = ((), (), s32[]{:S(2)}) async-start(), calls=%async_computation.2 | async-start | bytes 20971520 | tf_op jit(solution)/shard_map/all_gather | solution.py:175
  145.9 5.0 copy-start.3
  145.9 5.9 copy-start.7
  154.3 13.9 %copy-start.15 = (bf16[1024,2048]{1,0:T(8,128)(2,1)S(1)}, bf16[1024,2048]{1,0:T(8,128)(2,1)}, u32[]{:S(2)}) copy-start(bf16[1024,2048]{1,0:T(8,128)(2,1)} %param.33) | copy-start | bytes 12582916
  187.4 2.0 copy-start.45
  202.2 391.9 %all-reduce.14.cloned.1.call-start = ((), (), s32[]{:S(2)}) async-start(), calls=%async_computation.4 | async-start | bytes 16777216 | tf_op jit(solution)/shard_map/psum | solution.py:159
  371.7 7.2 copy-start.4
  371.7 7.3 copy-start.8
  371.7 8.3 copy-start.9
  379.0 6.6 copy-start.16
  380.1 15.3 %slice-start = ((s8[8388608]{0:T(1024)(128)(4,1)}), s8[4194304]{0:T(1024)(128)(4,1)S(1)}, s32[]{:S(2)}) async-start(s8[8388608]{0:T(1024)(128)(4,1)} %bitcast.108), calls=%async_computation.5 | async-start | bytes 8388608
  385.6 9.8 slice-start.1
  391.9 3.4 copy-start.10
  395.4 9.3 slice-start.2
  397.4 5.8 copy-start.12
  397.4 7.3 slice-start.3
  409.9 3.3 copy-start.14
  409.9 3.3 copy-start.26
  412.3 2.4 copy-start.21
  412.4 2.5 copy-start.44
  414.7 2.6 copy-start.23
  420.7 590.4 %all-reduce.12.cloned.1.call-start = ((), (), s32[]{:S(2)}) async-start(), calls=%async_computation.3 | async-start | bytes 41943040 | tf_op jit(solution)/shard_map/psum | solution.py:224
  420.7 15.8 %copy-start.17 = (bf16[1024,2048]{1,0:T(8,128)(2,1)S(1)}, bf16[1024,2048]{1,0:T(8,128)(2,1)}, u32[]{:S(2)}) copy-start(bf16[1024,2048]{1,0:T(8,128)(2,1)} %param.33) | copy-start | bytes 12582916
  420.7 39.5 %slice-start.4 = ((s8[8388608]{0:T(1024)(128)(4,1)}), s8[4194304]{0:T(1024)(128)(4,1)S(1)}, s32[]{:S(2)}) async-start(s8[8388608]{0:T(1024)(128)(4,1)} %bitcast.113), calls=%async_computation.9 | async-start | bytes 8388608
  436.5 20.0 %copy-start.19 = (bf16[1024,2048]{1,0:T(8,128)(2,1)S(1)}, bf16[1024,2048]{1,0:T(8,128)(2,1)}, u32[]{:S(2)}) copy-start(bf16[1024,2048]{1,0:T(8,128)(2,1)} %copy-done.18) | copy-start | bytes 12582916
  436.5 23.8 %slice-start.5 = ((s8[8388608]{0:T(1024)(128)(4,1)}), s8[4194304]{0:T(1024)(128)(4,1)S(1)}, s32[]{:S(2)}) async-start(s8[8388608]{0:T(1024)(128)(4,1)} %bitcast.113), calls=%async_computation.10 | async-start | bytes 8388608
  456.5 3.8 copy-start.25
  464.0 0.7 copy-start.41
  464.0 687.1 %all-reduce.10.cloned.1.call-start = ((), (), s32[]{:S(2)}) async-start(), calls=%async_computation.1 | async-start | bytes 4194304 | tf_op jit(solution)/shard_map/psum | solution.py:209
  509.6 84.5 %copy-start.28 = (f32[2048]{0:T(1024)S(1)}, f32[2048]{0:T(1024)}, u32[]{:S(2)}) copy-start(f32[2048]{0:T(1024)} %copy-done.27) | copy-start | bytes 24580
  509.6 84.5 %copy-start.30 = (f32[1024]{0:T(1024)S(1)}, f32[1024]{0:T(1024)}, u32[]{:S(2)}) copy-start(f32[1024]{0:T(1024)} %copy-done.29) | copy-start | bytes 12292
  519.8 81.7 %copy-start.34 = (f32[1024]{0:T(1024)S(1)}, f32[1024]{0:T(1024)}, u32[]{:S(2)}) copy-start(f32[1024]{0:T(1024)} %copy-done.33) | copy-start | bytes 12292
  519.8 81.7 %copy-start.32 = (f32[1024]{0:T(1024)S(1)}, f32[1024]{0:T(1024)}, u32[]{:S(2)}) copy-start(f32[1024]{0:T(1024)} %copy-done.31) | copy-start | bytes 12292
  598.6 9.2 copy-start.42
  1031.3 122.8 %copy-start.1 = (bf16[512,2048]{1,0:T(8,128)(2,1)S(1)}, bf16[512,2048]{1,0:T(8,128)(2,1)}, u32[]{:S(2)}) copy-start(bf16[512,2048]{1,0:T(8,128)(2,1)} %param.25) | copy-start | bytes 6291460
Sparse Core Ops, SparseCore 0:
  39.6 106.3 all-reduce.7
  202.3 157.2 all-gather.2
  420.8 173.2 all-reduce.13
  598.0 413.0 all-reduce.11
  1016.2 134.7 all-reduce.9
